TPU v7x, 256 devices: a whole 4x4x8 slice. The times are simulated.
256 devices in a mesh: replica: 32 (over y, z), shard: 8 (over x, core).
Axes of the slice: x: 4, y: 4, z: 8, core: 2. Of those that a mesh axis runs over, the one named last changes fastest.
Arguments:
- outer_params: float32 [1024, 4096], P('shard'), may hold values from -6 to 6, as said below
- local_params: bfloat16 [32, 1024, 4096], P('replica', 'shard'), may hold values from -70 to 70
- momentum: float32 [1024, 4096], P('shard'), may hold values from -6 to 6
Outputs:
- params_next: float32 [1024, 4096], P('shard')
- momentum_next: float32 [1024, 4096], P('shard')
- block_scales: float32 [32, 1024], P(None, 'shard')
Inputs may be any that keep to these rules, and one draw needn't show every extreme that they name: `outer_params`: outer parameters of order one.
All inputs are finite; a program needn't handle non-finite values.
Results may differ from a plain program's by a relative error of at most 0.005.
Values may be sent and summed in bfloat16 or wider, within the bound.
A program may use at most 64 MiB of HBM per device.

v0:
```python
import math
import jax
import jax.numpy as jnp
from jax import lax
from jax.sharding import Mesh
from jax.sharding import PartitionSpec as P

BLOCK = 128
REPLICA = ("replica_0", "replica_1")
REPLICA_SHARD = ("replica_0", "replica_1", "shard_0", "shard_1")
SHARD = ("shard_0", "shard_1")
epsilon = 1e-06
clip_level = 0.5
outer_rate = 0.7
outer_decay = 0.9
grid_levels = 7.0


def copy_for_each(x, axis):
    copies = jnp.broadcast_to(x, (lax.axis_size(axis), *x.shape))
    return lax.all_to_all(copies, axis, split_axis=0, concat_axis=0, tiled=True)


def taken_together(x, axis):
    everything = copy_for_each(x, axis)
    return jnp.max(everything, axis=0)


def in_blocks(x, dim, devices):
    dims = x.shape
    pieces = x.reshape(*dims[:dim], devices, dims[dim] // devices, *dims[dim + 1 :])
    return jnp.moveaxis(pieces, dim, 0)


def summed_on_arrival(x, axis, dim):
    pieces = in_blocks(x, dim, lax.axis_size(axis))
    arrived = lax.all_to_all(pieces, axis, split_axis=0, concat_axis=0, tiled=True)
    return arrived.astype(jnp.float32).sum(axis=0)


def over_axes(x, axes):
    for axis in axes:
        x = lax.psum(x, axis)
    return x


def smooth_step(values):
    return values - jnp.sin(2.0 * math.pi * values) / (2.0 * math.pi)


def smooth_round(values):
    return smooth_step(smooth_step(values))


def block_max(values):
    return jnp.max(
        jnp.abs(values).reshape(values.shape[0], values.shape[1] // BLOCK, BLOCK), axis=2
    )


def per_device(outer_params, local_params, momentum):
    workers = lax.axis_size(REPLICA)
    row_count = outer_params.shape[0]
    col_count = outer_params.shape[1]
    deltas = outer_params - local_params[0].astype(jnp.float32)
    absmax = taken_together(block_max(deltas), REPLICA)
    spread_scale = jnp.repeat(absmax + epsilon, BLOCK, axis=1)
    encoded = smooth_round(grid_levels * deltas / spread_scale).astype(jnp.bfloat16)
    summed_rows = summed_on_arrival(
        (spread_scale * encoded.astype(jnp.float32) / grid_levels).astype(jnp.bfloat16), REPLICA, 0
    )
    gradient_slice = summed_rows / workers
    square_total = over_axes(jnp.sum(gradient_slice * gradient_slice), REPLICA_SHARD)
    entry_count = row_count * lax.axis_size(SHARD) * col_count
    root_mean = jnp.sqrt(square_total / entry_count + epsilon)
    factor = jnp.minimum(1.0, clip_level / root_mean)
    gradient = lax.all_gather(gradient_slice, REPLICA, axis=0, tiled=True)
    clipped = factor * gradient
    momentum_next = outer_decay * momentum + clipped
    params_next = outer_params - outer_rate * (clipped + outer_decay * momentum_next)
    return (params_next, momentum_next, absmax.T)


def solution(mesh):
    finer = Mesh(mesh.devices.reshape(4, 8, 4, 2), ("replica_0", "replica_1", "shard_0", "shard_1"))
    placed = (P(SHARD, None), P(REPLICA, SHARD, None), P(SHARD, None))
    return jax.shard_map(
        per_device,
        mesh=finer,
        in_specs=placed,
        out_specs=(P(SHARD, None), P(SHARD, None), P(None, SHARD)),
        check_vma=False,
    )
```

profile of v0, /device:TPU:2, one launch (start us, length us, event | category | flops | bytes accessed | tf_op | source)
XLA Modules:
  0.0 185.8 jit_solution(7357414329227839950)
XLA Ops:
  7.2 0.0 all-gather.3.cloned.1.call-start
  7.2 2.1 %abs_bitcast_fusion = f32[16,8,32,128]{3,1,2,0:T(8,128)S(1)} fusion(f32[128,4096]{1,0:T(8,128)} %param.3, bf16[1,128,4096]{2,1,0:T(8,128)(2,1)} %param.4), kind=kLoop, calls=%fused_computation.9 | loop fusion | flops 1572864 | bytes 5242880
  9.3 0.4 copy.10
  9.7 0.6 reduce_max.18
  10.3 0.1 copy.8
  10.4 0.0 copy-start
  10.4 0.0 copy-start.1
  10.4 0.1 broadcast_in_dim.6
  10.5 28.4 %all_to_all.10 = f32[32,128,32]{1,2,0:T(8,128)} all-to-all(f32[32,128,32]{1,2,0:T(8,128)S(1)} %broadcast_in_dim.6), channel_id=1, replica_groups=mesh['replica_0'=4,'replica_1'=8,'shard_0'=4,'shard_1'=2] {'replica_0','..., dimensions={0} | all-to-all | bytes 1048576 | tf_op jit(solution)/shard_map/all_to_all | solution.py:21
  38.8 1.1 reduce_max.19
  39.9 0.0 copy-start.2
  39.9 0.1 copy.9
  40.0 0.6 broadcast_in_dim.7
  40.6 0.0 copy-done
  40.6 0.0 copy-done.1
  40.6 15.7 %fusion.1 = bf16[128,4096]{1,0:T(8,128)(2,1)} fusion(f32[16,8,32,128]{3,2,1,0:T(8,128)S(1)} %bitcast.24, f32[128,4096]{1,0:T(8,128)S(1)} %copy-done, bf16[1,128,4096]{2,1,0:T(8,128)(2,1)S(1)} %copy-done.1), kind=kLoop, calls=%fused_computation.3 | loop fusion | flops 7864320 | bytes 6291456 | tf_op jit(solution)/shard_map/convert_element_type | solution.py:70
  56.4 0.0 copy-done.2
  56.4 1.5 reshape.19
  57.9 33.7 %all_to_all.11 = bf16[32,4,4096]{2,1,0:T(4,128)(2,1)S(1)} all-to-all(bf16[32,4,4096]{2,1,0:T(4,128)(2,1)S(1)} %reshape.19), channel_id=1, replica_groups=mesh['replica_0'=4,'replica_1'=8,'shard_0'=4,'shard_1'=2] {'replica_0','..., dimensions={0} | all-to-all | bytes 2097152 | tf_op jit(solution)/shard_map/all_to_all | solution.py:37
  91.5 0.4 convert_reduce_fusion
  92.0 1.2 multiply_reduce_fusion
  93.2 0.0 all-gather.3.cloned.1.call-update
  93.2 9.2 %psum.28 = f32[]{:T(128)} all-reduce(f32[]{:T(128)} %get-tuple-element.5), channel_id=1, replica_groups=mesh['replica_0'=4,'replica_1'=8,'shard_0'=4,'shard_1'=2] {'replica_0'}, use_global_device_ids=true, to_apply=%region_4.0 | all-reduce | flops 1 | bytes 8 | tf_op jit(solution)/shard_map/psum | solution.py:43
  102.4 16.8 %psum.29 = f32[]{:T(128)} all-reduce(f32[]{:T(128)} %psum.28), channel_id=1, replica_groups=mesh['replica_0'=4,'replica_1'=8,'shard_0'=4,'shard_1'=2] {'replica_1'}, use_global_device_ids=true, to_apply=%region_5.0 | all-reduce | flops 1 | bytes 8 | tf_op jit(solution)/shard_map/psum | solution.py:43
  119.2 9.2 %psum.30 = f32[]{:T(128)} all-reduce(f32[]{:T(128)} %psum.29), channel_id=1, replica_groups=mesh['replica_0'=4,'replica_1'=8,'shard_0'=4,'shard_1'=2] {'shard_0'}, use_global_device_ids=true, to_apply=%region_6.0 | all-reduce | flops 1 | bytes 8 | tf_op jit(solution)/shard_map/psum | solution.py:43
  128.4 3.1 %psum.31 = f32[]{:T(128)} all-reduce(f32[]{:T(128)} %psum.30), channel_id=1, replica_groups=mesh['replica_0'=4,'replica_1'=8,'shard_0'=4,'shard_1'=2] {'shard_1'}, use_global_device_ids=true, to_apply=%region_7.0 | all-reduce | flops 1 | bytes 8 | tf_op jit(solution)/shard_map/psum | solution.py:43
  132.2 35.7 %all-gather.3.cloned.1.call-done = f32[32,4,4096]{2,1,0:T(4,128)} async-done(((f32[1,4,4096]{2,1,0:T(4,128)}), f32[32,4,4096]{2,1,0:T(4,128)}) %all-gather.3.cloned.1.call-update) | async-done | bytes 2097168 | tf_op jit(solution)/shard_map/all_gather | solution.py:77
  167.9 3.1 %broadcast_multiply_fusion = f32[16,8,4096]{2,1,0:T(8,128)} fusion(f32[16,8,4096]{2,1,0:T(8,128)} %bitcast.27, f32[]{:T(128)S(6)} %min_shard_map.3), kind=kLoop, calls=%fused_computation.10 | loop fusion | flops 524288 | bytes 4194308 | tf_op jit(solution)/shard_map/mul | solution.py:78
  171.0 2.9 %reshape.24 = f32[128,4096]{1,0:T(8,128)} reshape(f32[32,4,4096]{2,1,0:T(4,128)} %bitcast.25) | data formatting | bytes 4194304 | tf_op jit(solution)/shard_map/mul | solution.py:78
  173.9 5.0 %multiply_subtract_fusion = (f32[128,4096]{1,0:T(8,128)}, f32[128,4096]{1,0:T(8,128)}) fusion(f32[128,4096]{1,0:T(8,128)S(1)} %copy-done, f32[128,4096]{1,0:T(8,128)} %reshape.24, f32[128,4096]{1,0:T(8,128)} %param.5), kind=kLoop, calls=%fused_computation.5 | loop fusion | flops 3145728 | bytes 10485760 | tf_op jit(solution)/shard_map/sub | solution.py:80
  (1 shorter events, 0.0 us)
Async XLA Ops:
  7.2 160.7 %all-gather.3.cloned.1.call-start = ((), (), s32[]{:S(2)}) async-start(), calls=%async_computation.2 | async-start | bytes 2162688 | tf_op jit(solution)/shard_map/all_gather | solution.py:77
  10.4 30.3 %copy-start = (f32[128,4096]{1,0:T(8,128)S(1)}, f32[128,4096]{1,0:T(8,128)}, u32[]{:S(2)}) copy-start(f32[128,4096]{1,0:T(8,128)} %param.3) | copy-start | bytes 6291460
  10.4 30.3 %copy-start.1 = (bf16[1,128,4096]{2,1,0:T(8,128)(2,1)S(1)}, bf16[1,128,4096]{2,1,0:T(8,128)(2,1)}, u32[]{:S(2)}) copy-start(bf16[1,128,4096]{2,1,0:T(8,128)(2,1)} %param.4) | copy-start | bytes 3145732
  39.9 16.5 %copy-start.2 = (f32[128,32]{0,1:T(8,128)}, f32[128,32]{0,1:T(8,128)S(1)}, u32[]{:S(2)}) copy-start(f32[128,32]{0,1:T(8,128)S(1)} %reduce_max.19) | copy-start | bytes 49156
Sparse Core Ops, SparseCore 0:
  93.4 74.4 all-gather.2
where the time goes:
time: 186 us
  blocking collectives  100 us (54%)
  waiting for transfers between devices  35.7 us (19%)
  other arithmetic  29.4 us (16%)
  between operations  14.8 us (8%)
  local copies, waits for them, and re-layouts  5.59 us (3%)
    psum x4, blocking collectives, over_axes(): x = lax.psum(x, axis)  38.2 us
    all_gather x1, waiting for transfers between devices, per_device(): gradient = lax.all_gather(gradient_slice, REPLICA, axis=0, tiled=True)  35.7 us
    all_to_all x1, blocking collectives, summed_on_arrival(): lax.all_to_all(pieces, axis, split_axis=0, concat_axis=0, tiled=True)  33.7 us
    all_to_all x1, blocking collectives, copy_for_each(): return lax.all_to_all(copies, axis, split_axis=0, concat_axis=0, tiled=True)  28.4 us
    convert_element_type x1, other arithmetic, per_device(): (spread_scale * encoded.astype(jnp.float32) / grid_levels).astype(jnp.bfl...  15.7 us
    sub x1, other arithmetic, per_device(): outer_params - outer_rate * (clipped + outer_decay * momentum_next)  5.05 us
  transfers between devices with their start and end apart: 1, of which 1 were waited for; matrix products, arithmetic and copies ran while one was open for 0% of the time, Pallas kernels for 0%

commit v1 on v0

--- a/solution.py
+++ b/solution.py
@@ -74,7 +74,9 @@
     entry_count = row_count * lax.axis_size(SHARD) * col_count
     root_mean = jnp.sqrt(square_total / entry_count + epsilon)
     factor = jnp.minimum(1.0, clip_level / root_mean)
-    gradient = lax.all_gather(gradient_slice, REPLICA, axis=0, tiled=True)
+    gradient = jnp.concatenate(
+        lax.all_to_all(jnp.stack([gradient_slice] * lax.axis_size(REPLICA)), REPLICA, 0, 0), axis=0
+    )
     clipped = factor * gradient
     momentum_next = outer_decay * momentum + clipped
     params_next = outer_params - outer_rate * (clipped + outer_decay * momentum_next)

time: 186 us -> 178 us (0.957); the launches traced: 186 us -> 174 us
  waiting for transfers between devices: 35.7 us -> 0.01 us
  blocking collectives: 100 us -> 132 us
  between operations: 14.8 us -> 1.41 us
  starting transfers between devices: 0.04 us -> 5.04 us
    all_gather x1 -> x0, waiting for transfers between devices: 35.7 us -> none  [per_device(): gradient = lax.all_gather(gradient_slice, REPLICA, axis=0, tiled=True)]
    psum x4, blocking collectives: 38.2 us -> 69.6 us  [over_axes(): x = lax.psum(x, axis)]
    all_to_all x0 -> x1, starting transfers between devices: none -> 5.04 us  [per_device(): lax.all_to_all(jnp.stack([gradient_slice] * lax.axis_size(REPLICA)), REPL...]
  transfers between devices with their start and end apart: 1 -> 1, of which waited for: 1 -> 0; matrix products, arithmetic and copies ran while one was open for 0% -> 0% of each run, Pallas kernels for 0% -> 0%
where the time goes in v1:
time: 178 us; the launch traced here: 174 us
  blocking collectives  132 us (74%)
  other arithmetic  28.6 us (16%)
  local copies, waits for them, and re-layouts  7.38 us (4%)
  starting transfers between devices  5.04 us (3%)
    psum x4, blocking collectives, over_axes(): x = lax.psum(x, axis)  69.6 us
    all_to_all x1, blocking collectives, summed_on_arrival(): lax.all_to_all(pieces, axis, split_axis=0, concat_axis=0, tiled=True)  33.7 us
    all_to_all x1, blocking collectives, copy_for_each(): return lax.all_to_all(copies, axis, split_axis=0, concat_axis=0, tiled=True)  28.4 us
    convert_element_type x1, other arithmetic, per_device(): (spread_scale * encoded.astype(jnp.float32) / grid_levels).astype(jnp.bfl...  15.7 us
    all_to_all x1, starting transfers between devices, per_device(): lax.all_to_all(jnp.stack([gradient_slice] * lax.axis_size(REPLICA)), REPL...  5.04 us
    sub x1, other arithmetic, per_device(): outer_params - outer_rate * (clipped + outer_decay * momentum_next)  4.86 us
  transfers between devices with their start and end apart: 1, of which 0 were waited for; matrix products, arithmetic and copies ran while one was open for 0% of the time, Pallas kernels for 0%

profile of v1, /device:TPU:2, one launch (start us, length us, event | category | flops | bytes accessed | tf_op | source)
XLA Modules:
  0.0 174.1 jit_solution(10618491171491076700)
XLA Ops:
  0.6 2.1 %abs_bitcast_fusion = f32[16,8,32,128]{3,1,2,0:T(8,128)S(1)} fusion(f32[128,4096]{1,0:T(8,128)} %param.3, bf16[1,128,4096]{2,1,0:T(8,128)(2,1)} %param.4), kind=kLoop, calls=%fused_computation.9 | loop fusion | flops 1572864 | bytes 5242880
  2.7 0.4 copy.10
  3.1 0.6 reduce_max.18
  3.7 0.1 copy.8
  3.8 0.0 copy-start
  3.8 0.0 copy-start.1
  3.8 0.1 broadcast_in_dim.6
  3.9 28.4 %all_to_all.15 = f32[32,128,32]{1,2,0:T(8,128)} all-to-all(f32[32,128,32]{1,2,0:T(8,128)S(1)} %broadcast_in_dim.6), channel_id=1, replica_groups=mesh['replica_0'=4,'replica_1'=8,'shard_0'=4,'shard_1'=2] {'replica_0','..., dimensions={0} | all-to-all | bytes 1048576 | tf_op jit(solution)/shard_map/all_to_all | solution.py:21
  32.2 1.1 reduce_max.19
  33.3 0.0 copy-start.2
  33.3 0.1 copy.9
  33.4 0.6 broadcast_in_dim.7
  34.0 0.0 copy-done
  34.1 0.0 copy-done.1
  34.1 15.7 %fusion.1 = bf16[128,4096]{1,0:T(8,128)(2,1)} fusion(f32[16,8,32,128]{3,2,1,0:T(8,128)S(1)} %bitcast.22, f32[128,4096]{1,0:T(8,128)S(1)} %copy-done, bf16[1,128,4096]{2,1,0:T(8,128)(2,1)S(1)} %copy-done.1), kind=kLoop, calls=%fused_computation.3 | loop fusion | flops 7864320 | bytes 6291456 | tf_op jit(solution)/shard_map/convert_element_type | solution.py:70
  49.8 0.0 copy-done.2
  49.8 1.5 reshape.24
  51.3 33.7 %all_to_all.16 = bf16[32,4,4096]{2,1,0:T(4,128)(2,1)S(1)} all-to-all(bf16[32,4,4096]{2,1,0:T(4,128)(2,1)S(1)} %reshape.24), channel_id=1, replica_groups=mesh['replica_0'=4,'replica_1'=8,'shard_0'=4,'shard_1'=2] {'replica_0','..., dimensions={0} | all-to-all | bytes 2097152 | tf_op jit(solution)/shard_map/all_to_all | solution.py:37
  85.0 0.4 convert_reduce_fusion
  85.4 0.6 multiply_reduce_fusion
  86.0 1.8 %stack.2 = f32[32,4,4096]{2,1,0:T(4,128)} broadcast(f32[4,4096]{1,0:T(4,128)S(1)} %get-tuple-element.6), dimensions={1,2} | broadcast | bytes 2162688 | tf_op jit(solution)/shard_map/stack | solution.py:78
  87.8 5.0 %all-to-all-start.2 = ((f32[32,4,4096]{2,1,0:T(4,128)}), f32[32,4,4096]{2,1,0:T(4,128)}, u32[]{:S(2)}, u32[]{:S(2)}) async-start(f32[32,4,4096]{2,1,0:T(4,128)} %stack.2), calls=%async_computation.2 | async-start | bytes 4194304 | tf_op jit(solution)/shard_map/all_to_all | solution.py:78
  92.9 11.8 %psum.28 = f32[]{:T(128)} all-reduce(f32[]{:T(128)} %get-tuple-element.5), channel_id=1, replica_groups=mesh['replica_0'=4,'replica_1'=8,'shard_0'=4,'shard_1'=2] {'replica_0'}, use_global_device_ids=true, to_apply=%region_4.0 | all-reduce | flops 1 | bytes 8 | tf_op jit(solution)/shard_map/psum | solution.py:43
  104.6 45.5 %psum.29 = f32[]{:T(128)} all-reduce(f32[]{:T(128)} %psum.28), channel_id=1, replica_groups=mesh['replica_0'=4,'replica_1'=8,'shard_0'=4,'shard_1'=2] {'replica_1'}, use_global_device_ids=true, to_apply=%region_5.0 | all-reduce | flops 1 | bytes 8 | tf_op jit(solution)/shard_map/psum | solution.py:43
  150.2 9.2 %psum.30 = f32[]{:T(128)} all-reduce(f32[]{:T(128)} %psum.29), channel_id=1, replica_groups=mesh['replica_0'=4,'replica_1'=8,'shard_0'=4,'shard_1'=2] {'shard_0'}, use_global_device_ids=true, to_apply=%region_6.0 | all-reduce | flops 1 | bytes 8 | tf_op jit(solution)/shard_map/psum | solution.py:43
  159.4 3.1 %psum.31 = f32[]{:T(128)} all-reduce(f32[]{:T(128)} %psum.30), channel_id=1, replica_groups=mesh['replica_0'=4,'replica_1'=8,'shard_0'=4,'shard_1'=2] {'shard_1'}, use_global_device_ids=true, to_apply=%region_7.0 | all-reduce | flops 1 | bytes 8 | tf_op jit(solution)/shard_map/psum | solution.py:43
  163.2 0.0 all-to-all-done.2
  163.2 3.1 %broadcast_multiply_fusion = f32[16,8,4096]{2,1,0:T(8,128)} fusion(f32[16,8,4096]{2,1,0:T(8,128)} %bitcast.20, f32[]{:T(128)S(6)} %min_shard_map.3), kind=kLoop, calls=%fused_computation.10 | loop fusion | flops 524288 | bytes 4194308 | tf_op jit(solution)/shard_map/mul | solution.py:80
  166.3 2.9 %mul.43 = f32[128,4096]{1,0:T(8,128)} reshape(f32[32,4,4096]{2,1,0:T(4,128)} %bitcast.23) | data formatting | bytes 4194304 | tf_op jit(solution)/shard_map/mul | solution.py:80
  169.2 4.9 %multiply_subtract_fusion = (f32[128,4096]{1,0:T(8,128)}, f32[128,4096]{1,0:T(8,128)}) fusion(f32[128,4096]{1,0:T(8,128)S(1)} %copy-done, f32[128,4096]{1,0:T(8,128)} %mul.43, f32[128,4096]{1,0:T(8,128)} %param.5), kind=kLoop, calls=%fused_computation.5 | loop fusion | flops 3145728 | bytes 10485760 | tf_op jit(solution)/shard_map/sub | solution.py:82
  (1 shorter events, 0.0 us)
Async XLA Ops:
  3.8 30.3 %copy-start = (f32[128,4096]{1,0:T(8,128)S(1)}, f32[128,4096]{1,0:T(8,128)}, u32[]{:S(2)}) copy-start(f32[128,4096]{1,0:T(8,128)} %param.3) | copy-start | bytes 6291460
  3.8 30.3 %copy-start.1 = (bf16[1,128,4096]{2,1,0:T(8,128)(2,1)S(1)}, bf16[1,128,4096]{2,1,0:T(8,128)(2,1)}, u32[]{:S(2)}) copy-start(bf16[1,128,4096]{2,1,0:T(8,128)(2,1)} %param.4) | copy-start | bytes 3145732
  33.3 16.5 %copy-start.2 = (f32[128,32]{0,1:T(8,128)}, f32[128,32]{0,1:T(8,128)S(1)}, u32[]{:S(2)}) copy-start(f32[128,32]{0,1:T(8,128)S(1)} %reduce_max.19) | copy-start | bytes 49156
  87.8 75.3 %all-to-all-start.2 = ((f32[32,4,4096]{2,1,0:T(4,128)}), f32[32,4,4096]{2,1,0:T(4,128)}, u32[]{:S(2)}, u32[]{:S(2)}) async-start(f32[32,4,4096]{2,1,0:T(4,128)} %stack.2), calls=%async_computation.2 | async-start | bytes 4194304 | tf_op jit(solution)/shard_map/all_to_all | solution.py:78
